TPU v7x, 32 devices: a whole 2x2x4 slice. The times are simulated.
32 devices in a mesh: groups: 2 (over y), range: 8 (over z, x), sub: 2 (over core).
Axes of the slice: x: 2, y: 2, z: 4, core: 2. Of those that a mesh axis runs over, the one named last changes fastest.
Arguments:
- samples: float32 [2, 1024, 32, 128], P(None, ('groups', 'range', 'sub')), parts along dimension 1, may hold values from -6 to 6
- beam_weights: float32 [32, 8, 2, 64, 128], P(('groups', 'range'), None, None, None, 'sub'), parts along dimension 0, may hold values from -0.25 to 0.25
- subarrays: int32 [32, 8, 64], P(('groups', 'range', 'sub')), parts along dimension 0, may hold values from 0 to 511, as said below
- training: int32 [64], P(('groups', 'range', 'sub')), parts along dimension 0, may hold values 0 or 1
Outputs:
- covariance: float32 [32, 8, 64, 128], P(('groups', 'range', 'sub')), parts along dimension 0
- filtered: float32 [2, 128, 64, 128], P(None, None, ('groups', 'range', 'sub')), parts along dimension 2
- energy: float32 [256], P('groups'), parts along dimension 0
There are 2 independent parts, one for each index of `groups`. A program takes and returns all parts, laid end to end along the dimension named above; each array names one. Nothing has to cross between parts.
Inputs may be any that keep to these rules, and one draw needn't show every extreme that they name: `subarrays`: in each gate block the 512 indices are all 512 channels, each once.
All inputs are finite; a program needn't handle non-finite values. No bound on the sum of `training` on one device may be relied on, other than what follows from the above.
Results may differ from a plain program's by a relative error of at most 0.0003.
Values sent between devices are 32-bit elements; how exact they have to be, the bound alone decides.
A program may use at most 64 MiB of HBM per device.

v0:
```python
import jax
import jax.numpy as jnp
from jax import lax
from jax.sharding import PartitionSpec as P

GB = 2
loading = 0.05


def block_terms(snaps, chosen, weights, masked, factor):
    highest = lax.Precision.HIGHEST
    picked = jnp.take(snaps, chosen, axis=1)
    real_part = picked[0]
    imag_part = picked[1]
    real_masked = real_part * masked
    imag_masked = imag_part * masked
    cov_real = (
        jnp.einsum("snx,smx->snm", real_masked, real_part, precision=highest)
        + jnp.einsum("snx,smx->snm", imag_masked, imag_part, precision=highest)
    ) * factor
    cov_imag = (
        jnp.einsum("snx,smx->snm", imag_masked, real_part, precision=highest)
        - jnp.einsum("snx,smx->snm", real_masked, imag_part, precision=highest)
    ) * factor
    w_real = weights[:, 0]
    w_imag = weights[:, 1]
    out_real = jnp.einsum("snk,snx->kx", w_real, real_part, precision=highest) + jnp.einsum(
        "snk,snx->kx", w_imag, imag_part, precision=highest
    )
    out_imag = jnp.einsum("snk,snx->kx", w_real, imag_part, precision=highest) - jnp.einsum(
        "snk,snx->kx", w_imag, real_part, precision=highest
    )
    prod_real = jnp.einsum("snm,smk->snk", cov_real, w_real, precision=highest) - jnp.einsum(
        "snm,smk->snk", cov_imag, w_imag, precision=highest
    )
    prod_imag = jnp.einsum("snm,smk->snk", cov_real, w_imag, precision=highest) + jnp.einsum(
        "snm,smk->snk", cov_imag, w_real, precision=highest
    )
    quadratic = jnp.sum(w_real * prod_real + w_imag * prod_imag, axis=(0, 1))
    inverse = 1.0 / jnp.sqrt(quadratic + loading)
    filtered = jnp.stack([out_real * inverse[:, None], out_imag * inverse[:, None]])
    energy = jnp.sum(out_real * out_real + out_imag * out_imag, axis=1)
    covariance = jnp.concatenate([cov_real, cov_imag], axis=-1)
    return (covariance, filtered, energy)


def body(samples, beam_weights, subarrays, training):
    range_count = lax.axis_size("range")
    core_count = lax.axis_size("sub")
    parts_iq, chan_dev, all_gates, pulses = samples.shape
    gate_dev = all_gates // (range_count * core_count)
    channels = chan_dev * range_count * core_count
    blocks_dev = gate_dev // GB
    spread = samples.reshape(parts_iq, 1, 1, chan_dev, range_count, core_count, gate_dev, pulses)
    turned = lax.all_to_all(
        lax.all_to_all(spread, "range", split_axis=4, concat_axis=1, tiled=True),
        "sub",
        split_axis=5,
        concat_axis=2,
        tiled=True,
    )
    local_data = turned.reshape(parts_iq, channels, blocks_dev, GB * pulses).transpose(2, 0, 1, 3)
    mine = lax.all_to_all(beam_weights, "sub", split_axis=0, concat_axis=4, tiled=True)
    gates_on = training.astype(jnp.float32).reshape(blocks_dev, GB)
    masked = jnp.repeat(gates_on, pulses, axis=1)
    factor = 1.0 / (GB * pulses)
    covs, filts, energies = jax.vmap(block_terms, in_axes=(0, 0, 0, 0, None))(
        local_data, subarrays, mine, masked, factor
    )
    beams = filts.shape[2]
    filtered = filts.reshape(blocks_dev, parts_iq, beams, GB, pulses).transpose(1, 2, 0, 3, 4)
    filtered = filtered.reshape(parts_iq, beams, gate_dev, pulses)
    total = lax.psum(jnp.sum(energies, axis=0), ("range", "sub"))
    energy = total / (all_gates * pulses)
    return (covs, filtered, energy)


def solution(mesh):
    placed = (
        P(None, ("groups", "range", "sub"), None, None),
        P(("groups", "range"), None, None, None, "sub"),
        P(("groups", "range", "sub"), None, None),
        P(("groups", "range", "sub")),
    )
    return jax.shard_map(
        body,
        mesh=mesh,
        in_specs=placed,
        out_specs=(
            P(("groups", "range", "sub"), None, None, None),
            P(None, None, ("groups", "range", "sub"), None),
            P("groups"),
        ),
        check_vma=False,
    )
```

profile of v0, /device:TPU:0, one launch (start us, length us, event | category | flops | bytes accessed | tf_op | source)
XLA Modules:
  0.0 92.5 jit_solution(9004139148378862796)
XLA Ops:
  0.6 0.0 copy-start
  0.6 2.5 %reshape.157 = f32[2,1,65536]{2,1,0:T(1,128)} reshape(f32[2,8,2,64,64]{4,3,2,1,0:T(8,128)} %param.5) | data formatting | bytes 1048576
  3.2 3.5 %all-to-all-start.2 = ((f32[2,1,65536]{2,1,0:T(1,128)}), f32[2,1,65536]{2,1,0:T(1,128)S(1)}, u32[]{:S(2)}, u32[]{:S(2)}) async-start(f32[2,1,65536]{2,1,0:T(1,128)} %reshape.157), calls=%async_computation.2 | async-start | bytes 1048576 | tf_op jit(solution)/shard_map/all_to_all | solution.py:63
  6.6 0.0 copy-done
  6.7 1.6 %copy.24 = f32[2,1,1,32,8,2,2,128]{7,6,3,5,0,2,1,4:T(2,128)} copy(f32[2,1,1,32,8,2,2,128]{7,6,5,4,3,0,2,1:T(2,128)S(1)} %bitcast.103) | data formatting | bytes 2097152 | tf_op jit(solution)/shard_map/reshape | solution.py:54
  8.2 0.0 copy-start.2
  8.2 0.2 all-to-all-done.2
  8.4 0.0 copy-start.1
  8.4 7.4 %all-to-all-start = ((f32[2,1,1,32,8,2,2,128]{7,6,3,5,0,2,1,4:T(2,128)}), f32[2,1,1,32,8,2,2,128]{7,6,3,5,0,2,1,4:T(2,128)S(1)}, u32[]{:S(2)}, u32[]{:S(2)}) async-start(f32[2,1,1,32,8,2,2,128]{7,6,3,5,0,2,1,4:T(2,128)} %copy.24), calls=%async_computation | async-start | bytes 2097152 | tf_op jit(solution)/shard_map/all_to_all | solution.py:56
  15.8 0.0 copy-done.2
  15.8 0.0 copy-done.1
  15.9 0.1 reshape.147
  15.9 0.5 broadcast.75
  16.4 2.3 %reduce.5 = f32[2,65536]{1,0:T(2,128)S(1)} reduce(f32[2,1,65536]{2,1,0:T(1,128)S(1)} %all-to-all-done.2, f32[]{:T(128)} %broadcast.75), dimensions={1}, to_apply=%all_to_all.44.reduce_sub_computation | reduce | bytes 1048580 | tf_op jit(solution)/shard_map/all_to_all | solution.py:63
  18.8 0.6 reshape.158
  19.4 1.9 %copy.29 = f32[1,8,2,64,2,64]{5,4,3,1,2,0:T(2,128)} copy(f32[1,8,2,64,2,64]{5,3,2,1,4,0:T(8,128)S(1)} %bitcast.98) | data formatting | bytes 1048576 | tf_op jit(solution)/shard_map/all_to_all | solution.py:63
  21.2 1.8 %all_to_all.47 = f32[1,8,2,64,128]{4,3,1,2,0:T(8,128)S(1)} reshape(f32[1,8,2,64,2,64]{5,4,3,1,2,0:T(2,128)} %copy.29) | data formatting | bytes 1048576 | tf_op jit(solution)/shard_map/all_to_all | solution.py:63
  23.1 0.1 broadcast_bitcast_fusion
  23.1 18.9 %all-to-all-done = f32[2,1,1,32,8,2,2,128]{7,6,3,5,0,2,1,4:T(2,128)S(1)} async-done(((f32[2,1,1,32,8,2,2,128]{7,6,3,5,0,2,1,4:T(2,128)}), f32[2,1,1,32,8,2,2,128]{7,6,3,5,0,2,1,4:T(2,128)S(1)}, u32[]{:S(2)}, u32[]{:S(2)}) %all-to-all-start) | async-done | bytes 1048608 | tf_op jit(solution)/shard_map/all_to_all | solution.py:56
  42.1 0.1 copy.25
  42.1 4.6 %all_to_all.51 = f32[2,8,1,32,1,2,2,128]{7,6,3,1,0,4,2,5:T(2,128)S(1)} all-to-all(f32[2,8,1,32,1,2,2,128]{7,6,3,1,0,4,2,5:T(2,128)S(1)} %copy.25), channel_id=1, replica_groups=mesh['groups'=2,'range'=8,'sub'=2] {'sub'}, dimensions={5} | all-to-all | bytes 2097152 | tf_op jit(solution)/shard_map/all_to_all | solution.py:55
  46.7 0.1 copy.26
  46.8 0.8 copy.27
  47.6 2.3 %gather_fusion = f32[512,2,256]{2,1,0:T(2,128)S(1)} fusion(f32[1,2,512,256]{3,1,2,0:T(2,128)S(1)} %copy.27, s32[512]{0:T(512)S(1)} %reshape.147), kind=kCustom, calls=%fused_computation | custom fusion | bytes 2101248 | tf_op jit(solution)/shard_map/vmap(jit(_take))/gather | solution.py:12
  50.0 0.1 copy.28
  50.1 0.1 broadcast_select_fusion
  50.2 1.0 %convolution_bitcast_fusion.2 = f32[256,128]{1,0:T(8,128)S(1)} fusion(f32[1,2,8,64,256]{4,3,2,1,0:T(8,128)S(1)} %broadcast_select_fusion, f32[1,8,2,64,128]{4,3,1,2,0:T(8,128)S(1)} %all_to_all.47), kind=kOutput, calls=%fused_computation.13 | convolution fusion | flops 201326592 | bytes 917504 | tf_op jit(solution)/shard_map/vmap(snk,snx->kx)/dot_general | solution.py:27
  51.2 1.0 %convolution_bitcast_fusion = f32[256,128]{1,0:T(8,128)S(1)} fusion(f32[1,2,8,64,256]{4,3,2,1,0:T(8,128)S(1)} %broadcast_select_fusion, f32[1,8,2,64,128]{4,3,1,2,0:T(8,128)S(1)} %all_to_all.47), kind=kOutput, calls=%fused_computation.11 | convolution fusion | flops 201326592 | bytes 917504 | tf_op jit(solution)/shard_map/vmap(snk,snx->kx)/dot_general | solution.py:30
  52.2 0.6 fusion.12
  52.9 0.6 fusion.2
  53.5 0.4 fusion.19
  53.9 0.4 fusion.18
  54.3 0.6 fusion.8
  54.9 1.0 %fusion.6 = f32[256,128]{1,0:T(8,128)S(1)} fusion(f32[256,128]{1,0:T(8,128)S(1)} %convolution_bitcast_fusion.2, f32[1,2,8,64,256]{4,3,2,1,0:T(8,128)S(1)} %broadcast_select_fusion, f32[1,8,2,64,128]{4,3,1,2,0:T(8,128)S(1)} %all_to_all.47), kind=kOutput, calls=%fused_computation.15 | convolution fusion | flops 201359360 | bytes 1048576 | tf_op jit(solution)/shard_map/vmap(snk,snx->kx)/dot_general | solution.py:27
  55.9 0.6 fusion.3
  56.5 0.4 fusion
  56.9 0.4 fusion.5
  57.4 1.0 %add_reduce_fusion = (f32[128]{0:T(128)S(1)}, f32[256,128]{1,0:T(8,128)S(1)}, f32[256,128]{1,0:T(8,128)S(1)}) fusion(f32[256,128]{1,0:T(8,128)S(1)} %fusion.6, f32[128]{0:T(128)S(1)} %add_rsqrt_fusion, f32[256,128]{1,0:T(8,128)S(1)} %convolution_bitcast_fusion, f32[1,8,2,64,128]{4,3,1,2,0:T(8,128)S(1)} %all_to_all.47, ...), kind=kOutput, calls=%fused_computation.36 | convolution fusion | flops 201555840 | bytes 1311744 | tf_op jit(solution)/shard_map/vmap(snk,snx->kx)/dot_general | solution.py:30
  58.4 31.6 %psum.7 = f32[128]{0:T(128)S(1)} all-reduce(f32[128]{0:T(128)S(1)} %get-tuple-element.3), channel_id=1, replica_groups=mesh['groups'=2,'range'=8,'sub'=2] {'range','sub'}, use_global_device_ids=true, to_apply=%region_2.3 | all-reduce | flops 128 | bytes 1024 | tf_op jit(solution)/shard_map/psum | solution.py:73
  90.1 0.5 broadcast_multiply_fusion.2
  90.6 0.1 copy.30
  90.7 0.1 copy.31
  90.8 0.8 pad_maximum_fusion
  91.7 0.8 pad_maximum_fusion.1
  (6 shorter events, 0.0 us)
Async XLA Ops:
  0.6 6.0 %copy-start = (f32[2,32,32,128]{3,2,1,0:T(8,128)S(1)}, f32[2,32,32,128]{3,2,1,0:T(8,128)}, u32[]{:S(2)}) copy-start(f32[2,32,32,128]{3,2,1,0:T(8,128)} %param.4) | copy-start | bytes 3145732
  3.2 5.2 %all-to-all-start.2 = ((f32[2,1,65536]{2,1,0:T(1,128)}), f32[2,1,65536]{2,1,0:T(1,128)S(1)}, u32[]{:S(2)}, u32[]{:S(2)}) async-start(f32[2,1,65536]{2,1,0:T(1,128)} %reshape.157), calls=%async_computation.2 | async-start | bytes 1048576 | tf_op jit(solution)/shard_map/all_to_all | solution.py:63
  8.2 7.6 %copy-start.2 = (s32[2]{0:T(128)S(1)}, s32[2]{0:T(128)}, u32[]{:S(2)}) copy-start(s32[2]{0:T(128)} %param.7) | copy-start | bytes 28
  8.4 7.4 %copy-start.1 = (s32[1,8,64]{2,1,0:T(8,128)S(1)}, s32[1,8,64]{2,1,0:T(8,128)}, u32[]{:S(2)}) copy-start(s32[1,8,64]{2,1,0:T(8,128)} %param.6) | copy-start | bytes 6148
  8.4 33.7 %all-to-all-start = ((f32[2,1,1,32,8,2,2,128]{7,6,3,5,0,2,1,4:T(2,128)}), f32[2,1,1,32,8,2,2,128]{7,6,3,5,0,2,1,4:T(2,128)S(1)}, u32[]{:S(2)}, u32[]{:S(2)}) async-start(f32[2,1,1,32,8,2,2,128]{7,6,3,5,0,2,1,4:T(2,128)} %copy.24), calls=%async_computation | async-start | bytes 2097152 | tf_op jit(solution)/shard_map/all_to_all | solution.py:56
where the time goes:
time: 92.9 us; the launch traced here: 92.5 us
  blocking collectives  36.2 us (39%)
  waiting for transfers between devices  19.1 us (21%)
  local copies, waits for them, and re-layouts  12.7 us (14%)
  starting transfers between devices  10.9 us (12%)
  matrix products  8.13 us (9%)
  other arithmetic  4.67 us (5%)
    psum x1, blocking collectives, body(): total = lax.psum(jnp.sum(energies, axis=0), ('range', 'sub'))  31.6 us
    all_to_all x1, waiting for transfers between devices, body(): lax.all_to_all(spread, 'range', split_axis=4, concat_axis=1, tiled=True)  18.9 us
    all_to_all x1, starting transfers between devices, body(): lax.all_to_all(spread, 'range', split_axis=4, concat_axis=1, tiled=True)  7.41 us
    all_to_all x1, blocking collectives, body(): lax.all_to_all(lax.all_to_all(spread, 'range', split_axis=4, concat_axis=...  4.58 us
    all_to_all x3, local copies, waits for them, and re-layouts, body(): lax.all_to_all(beam_weights, 'sub', split_axis=0, concat_axis=4, tiled=True)  4.18 us
    all_to_all x1, starting transfers between devices, body(): lax.all_to_all(beam_weights, 'sub', split_axis=0, concat_axis=4, tiled=True)  3.49 us
    unnamed x8, local copies, waits for them, and re-layouts  3.15 us
    gather x4, local copies, waits for them, and re-layouts, block_terms(): picked = jnp.take(snaps, chosen, axis=1)  2.5 us
  transfers between devices with their start and end apart: 2, of which 2 were waited for; matrix products, arithmetic and copies ran while one was open for 8% of the time, Pallas kernels for 0%

commit v1 on v0

--- a/solution.py
+++ b/solution.py
@@ -52,13 +52,10 @@
     channels = chan_dev * range_count * core_count
     blocks_dev = gate_dev // GB
     spread = samples.reshape(parts_iq, 1, 1, chan_dev, range_count, core_count, gate_dev, pulses)
-    turned = lax.all_to_all(
-        lax.all_to_all(spread, "range", split_axis=4, concat_axis=1, tiled=True),
-        "sub",
-        split_axis=5,
-        concat_axis=2,
-        tiled=True,
-    )
+    part = lax.all_to_all(spread, "range", split_axis=4, concat_axis=1, tiled=True)
+    pieces = jnp.split(part, lax.axis_size("sub"), axis=5)
+    got = lax.all_to_all(jnp.stack(pieces), "sub", 0, 0)
+    turned = jnp.concatenate(got, axis=2)
     local_data = turned.reshape(parts_iq, channels, blocks_dev, GB * pulses).transpose(2, 0, 1, 3)
     mine = lax.all_to_all(beam_weights, "sub", split_axis=0, concat_axis=4, tiled=True)
     gates_on = training.astype(jnp.float32).reshape(blocks_dev, GB)

time: 92.9 us -> 93.8 us (level)
  no operation moved by 1% of the time
where the time goes in v1:
time: 93.8 us; the launch traced here: 93.4 us
  blocking collectives  36.2 us (39%)
  waiting for transfers between devices  19.1 us (20%)
  local copies, waits for them, and re-layouts  12.8 us (14%)
  starting transfers between devices  10.9 us (12%)
  matrix products  8.13 us (9%)
  other arithmetic  5.43 us (6%)
    psum x1, blocking collectives, body(): total = lax.psum(jnp.sum(energies, axis=0), ('range', 'sub'))  31.6 us
    all_to_all x1, waiting for transfers between devices, body(): lax.all_to_all(spread, 'range', split_axis=4, concat_axis=1, tiled=True)  18.9 us
    all_to_all x1, starting transfers between devices, body(): lax.all_to_all(spread, 'range', split_axis=4, concat_axis=1, tiled=True)  7.41 us
    all_to_all x1, blocking collectives, body(): got = lax.all_to_all(jnp.stack(pieces), 'sub', 0, 0)  4.58 us
    all_to_all x3, local copies, waits for them, and re-layouts, body(): lax.all_to_all(beam_weights, 'sub', split_axis=0, concat_axis=4, tiled=True)  4.18 us
    all_to_all x1, starting transfers between devices, body(): lax.all_to_all(beam_weights, 'sub', split_axis=0, concat_axis=4, tiled=True)  3.49 us
    unnamed x8, local copies, waits for them, and re-layouts  3.15 us
    gather x4, local copies, waits for them, and re-layouts, block_terms(): picked = jnp.take(snaps, chosen, axis=1)  2.5 us
  transfers between devices with their start and end apart: 2, of which 2 were waited for; matrix products, arithmetic and copies ran while one was open for 8% of the time, Pallas kernels for 0%

profile of v1, /device:TPU:0, one launch (start us, length us, event | category | flops | bytes accessed | tf_op | source)
XLA Modules:
  0.0 93.4 jit_solution(11681672451801026995)
XLA Ops:
  0.6 0.0 copy-start
  0.6 2.5 %reshape.160 = f32[2,1,65536]{2,1,0:T(1,128)} reshape(f32[2,8,2,64,64]{4,3,2,1,0:T(8,128)} %param.5) | data formatting | bytes 1048576
  3.2 3.5 %all-to-all-start.2 = ((f32[2,1,65536]{2,1,0:T(1,128)}), f32[2,1,65536]{2,1,0:T(1,128)S(1)}, u32[]{:S(2)}, u32[]{:S(2)}) async-start(f32[2,1,65536]{2,1,0:T(1,128)} %reshape.160), calls=%async_computation.2 | async-start | bytes 1048576 | tf_op jit(solution)/shard_map/all_to_all | solution.py:60
  6.6 0.0 copy-done
  6.7 1.6 %copy.27 = f32[2,1,1,32,8,2,2,128]{7,6,3,0,5,2,1,4:T(2,128)} copy(f32[2,1,1,32,8,2,2,128]{7,6,5,4,3,0,2,1:T(2,128)S(1)} %bitcast.107) | data formatting | bytes 2097152 | tf_op jit(solution)/shard_map/reshape | solution.py:54
  8.2 0.0 copy-start.2
  8.2 0.1 all-to-all-done.2
  8.4 0.0 copy-start.1
  8.4 7.4 %all-to-all-start = ((f32[2,1,1,32,8,2,2,128]{7,6,3,0,5,2,1,4:T(2,128)}), f32[2,1,1,32,8,2,2,128]{7,6,3,0,5,2,1,4:T(2,128)S(1)}, u32[]{:S(2)}, u32[]{:S(2)}) async-start(f32[2,1,1,32,8,2,2,128]{7,6,3,0,5,2,1,4:T(2,128)} %copy.27), calls=%async_computation | async-start | bytes 2097152 | tf_op jit(solution)/shard_map/all_to_all | solution.py:55
  15.8 0.0 copy-done.2
  15.8 0.0 copy-done.1
  15.9 0.1 reshape.150
  15.9 0.5 broadcast.75
  16.4 2.3 %reduce.5 = f32[2,65536]{1,0:T(2,128)S(1)} reduce(f32[2,1,65536]{2,1,0:T(1,128)S(1)} %all-to-all-done.2, f32[]{:T(128)} %broadcast.75), dimensions={1}, to_apply=%all_to_all.34.reduce_sub_computation | reduce | bytes 1048580 | tf_op jit(solution)/shard_map/all_to_all | solution.py:60
  18.8 0.6 reshape.161
  19.4 1.9 %copy.33 = f32[1,8,2,64,2,64]{5,4,3,1,2,0:T(2,128)} copy(f32[1,8,2,64,2,64]{5,3,2,1,4,0:T(8,128)S(1)} %bitcast.102) | data formatting | bytes 1048576 | tf_op jit(solution)/shard_map/all_to_all | solution.py:60
  21.2 1.8 %all_to_all.37 = f32[1,8,2,64,128]{4,3,1,2,0:T(8,128)S(1)} reshape(f32[1,8,2,64,2,64]{5,4,3,1,2,0:T(2,128)} %copy.33) | data formatting | bytes 1048576 | tf_op jit(solution)/shard_map/all_to_all | solution.py:60
  23.1 0.1 broadcast_bitcast_fusion
  23.1 18.9 %all-to-all-done = f32[2,1,1,32,8,2,2,128]{7,6,3,0,5,2,1,4:T(2,128)S(1)} async-done(((f32[2,1,1,32,8,2,2,128]{7,6,3,0,5,2,1,4:T(2,128)}), f32[2,1,1,32,8,2,2,128]{7,6,3,0,5,2,1,4:T(2,128)S(1)}, u32[]{:S(2)}, u32[]{:S(2)}) %all-to-all-start) | async-done | bytes 1048608 | tf_op jit(solution)/shard_map/all_to_all | solution.py:55
  42.1 0.1 slice_bitcast_fusion.3
  42.1 0.8 pad_maximum_fusion
  42.9 0.1 copy.29
  43.0 4.6 %all_to_all.41 = f32[2,2,8,1,32,1,1,2,128]{8,7,3,4,2,1,6,5,0:T(2,128)S(1)} all-to-all(f32[2,2,8,1,32,1,1,2,128]{8,7,3,4,2,1,6,5,0:T(2,128)S(1)} %copy.29), channel_id=1, replica_groups=mesh['groups'=2,'range'=8,'sub'=2] {'sub'}, dimensions={0} | all-to-all | bytes 2097152 | tf_op jit(solution)/shard_map/all_to_all | solution.py:57
  47.6 0.1 copy.30
  47.7 0.8 copy.31
  48.5 2.3 %gather_fusion = f32[512,2,256]{2,1,0:T(2,128)S(1)} fusion(f32[1,2,512,256]{3,1,2,0:T(2,128)S(1)} %copy.31, s32[512]{0:T(512)S(1)} %reshape.150), kind=kCustom, calls=%fused_computation | custom fusion | bytes 2101248 | tf_op jit(solution)/shard_map/vmap(jit(_take))/gather | solution.py:12
  50.9 0.1 copy.32
  51.0 0.1 broadcast_select_fusion
  51.1 1.0 %convolution_bitcast_fusion.2 = f32[256,128]{1,0:T(8,128)S(1)} fusion(f32[1,2,8,64,256]{4,3,2,1,0:T(8,128)S(1)} %broadcast_select_fusion, f32[1,8,2,64,128]{4,3,1,2,0:T(8,128)S(1)} %all_to_all.37), kind=kOutput, calls=%fused_computation.13 | convolution fusion | flops 201326592 | bytes 917504 | tf_op jit(solution)/shard_map/vmap(snk,snx->kx)/dot_general | solution.py:27
  52.1 1.0 %convolution_bitcast_fusion = f32[256,128]{1,0:T(8,128)S(1)} fusion(f32[1,2,8,64,256]{4,3,2,1,0:T(8,128)S(1)} %broadcast_select_fusion, f32[1,8,2,64,128]{4,3,1,2,0:T(8,128)S(1)} %all_to_all.37), kind=kOutput, calls=%fused_computation.11 | convolution fusion | flops 201326592 | bytes 917504 | tf_op jit(solution)/shard_map/vmap(snk,snx->kx)/dot_general | solution.py:30
  53.1 0.6 fusion.12
  53.7 0.6 fusion.2
  54.4 0.4 fusion.19
  54.8 0.4 fusion.18
  55.2 0.6 fusion.8
  55.8 1.0 %fusion.6 = f32[256,128]{1,0:T(8,128)S(1)} fusion(f32[256,128]{1,0:T(8,128)S(1)} %convolution_bitcast_fusion.2, f32[1,2,8,64,256]{4,3,2,1,0:T(8,128)S(1)} %broadcast_select_fusion, f32[1,8,2,64,128]{4,3,1,2,0:T(8,128)S(1)} %all_to_all.37), kind=kOutput, calls=%fused_computation.15 | convolution fusion | flops 201359360 | bytes 1048576 | tf_op jit(solution)/shard_map/vmap(snk,snx->kx)/dot_general | solution.py:27
  56.8 0.6 fusion.3
  57.4 0.4 fusion
  57.8 0.4 fusion.5
  58.3 1.0 %add_reduce_fusion = (f32[128]{0:T(128)S(1)}, f32[256,128]{1,0:T(8,128)S(1)}, f32[256,128]{1,0:T(8,128)S(1)}) fusion(f32[256,128]{1,0:T(8,128)S(1)} %fusion.6, f32[128]{0:T(128)S(1)} %add_rsqrt_fusion, f32[256,128]{1,0:T(8,128)S(1)} %convolution_bitcast_fusion, f32[1,8,2,64,128]{4,3,1,2,0:T(8,128)S(1)} %all_to_all.37, ...), kind=kOutput, calls=%fused_computation.39 | convolution fusion | flops 201555840 | bytes 1311744 | tf_op jit(solution)/shard_map/vmap(snk,snx->kx)/dot_general | solution.py:30
  59.3 31.6 %psum.7 = f32[128]{0:T(128)S(1)} all-reduce(f32[128]{0:T(128)S(1)} %get-tuple-element.5), channel_id=1, replica_groups=mesh['groups'=2,'range'=8,'sub'=2] {'range','sub'}, use_global_device_ids=true, to_apply=%region_2.3 | all-reduce | flops 128 | bytes 1024 | tf_op jit(solution)/shard_map/psum | solution.py:70
  90.9 0.5 broadcast_multiply_fusion.2
  91.5 0.1 copy.34
  91.6 0.1 copy.35
  91.7 0.8 pad_maximum_fusion.1
  92.5 0.8 pad_maximum_fusion.2
  (6 shorter events, 0.0 us)
Async XLA Ops:
  0.6 6.0 %copy-start = (f32[2,32,32,128]{3,2,1,0:T(8,128)S(1)}, f32[2,32,32,128]{3,2,1,0:T(8,128)}, u32[]{:S(2)}) copy-start(f32[2,32,32,128]{3,2,1,0:T(8,128)} %param.4) | copy-start | bytes 3145732
  3.2 5.2 %all-to-all-start.2 = ((f32[2,1,65536]{2,1,0:T(1,128)}), f32[2,1,65536]{2,1,0:T(1,128)S(1)}, u32[]{:S(2)}, u32[]{:S(2)}) async-start(f32[2,1,65536]{2,1,0:T(1,128)} %reshape.160), calls=%async_computation.2 | async-start | bytes 1048576 | tf_op jit(solution)/shard_map/all_to_all | solution.py:60
  8.2 7.6 %copy-start.2 = (s32[2]{0:T(128)S(1)}, s32[2]{0:T(128)}, u32[]{:S(2)}) copy-start(s32[2]{0:T(128)} %param.7) | copy-start | bytes 28
  8.4 7.4 %copy-start.1 = (s32[1,8,64]{2,1,0:T(8,128)S(1)}, s32[1,8,64]{2,1,0:T(8,128)}, u32[]{:S(2)}) copy-start(s32[1,8,64]{2,1,0:T(8,128)} %param.6) | copy-start | bytes 6148
  8.4 33.7 %all-to-all-start = ((f32[2,1,1,32,8,2,2,128]{7,6,3,0,5,2,1,4:T(2,128)}), f32[2,1,1,32,8,2,2,128]{7,6,3,0,5,2,1,4:T(2,128)S(1)}, u32[]{:S(2)}, u32[]{:S(2)}) async-start(f32[2,1,1,32,8,2,2,128]{7,6,3,0,5,2,1,4:T(2,128)} %copy.27), calls=%async_computation | async-start | bytes 2097152 | tf_op jit(solution)/shard_map/all_to_all | solution.py:55
